TPU v7x, 32 devices: a whole 2x2x4 slice. The times are simulated.
32 devices in a mesh: grp: 2 (over x), pq: 16 (over z, y, core).
Axes of the slice: x: 2, y: 2, z: 4, core: 2. Of those that a mesh axis runs over, the one named last changes fastest.
Arguments:
- pair_blocks: bfloat16 [4, 288, 128, 128], P('grp', 'pq'), may hold values from -6 to 6
- block_list: int32 [4, 288], P('grp', 'pq'), may hold values from 0 to 2047, as said below
- block_count: int32 [4, 16], P('grp', 'pq'), may hold values from 1 to 18, as said below
- coef: bfloat16 [4096, 512], P('pq', 'grp'), may hold values from -0.09375 to 0.09375
Outputs:
- transformed: float32 [8, 512, 512], P('grp', 'pq')
Inputs may be any that keep to these rules, and one draw needn't show every extreme that they name: `block_list`: within one row the ids are distinct, each in 0 to 2 * 32^2 - 1. `block_count`: in every row some device has exactly 18 live slots.
All inputs are finite; a program needn't handle non-finite values.
Results may differ from a plain program's by a relative error of at most 0.0042.
Values may be sent and summed in bfloat16 or wider, within the bound.
A program may use at most 64 MiB of HBM per device.

v0:
```python
import jax
import jax.numpy as jnp
from jax import lax
from jax.sharding import PartitionSpec as P

KL_PANEL = 2


def partner(value, axis, distance):
    mask = 2**distance
    pairs = [(source, source ^ mask) for source in range(lax.axis_size(axis))]
    return lax.ppermute(value, axis, pairs)


def block_term(block, ident, coef_full, tile, nblk):
    per_kl = nblk * nblk
    which = ident // per_kl
    row_blk = ident // nblk % nblk
    col_blk = ident % nblk
    col_coef = lax.dynamic_slice_in_dim(coef_full, col_blk * tile, tile, 0)
    row_coef = lax.dynamic_slice_in_dim(coef_full, row_blk * tile, tile, 0)
    half = jnp.dot(block, col_coef, preferred_element_type=jnp.float32).astype(jnp.bfloat16)
    term = lax.dot_general(
        row_coef, half, (((0,), (0,)), ((), ())), preferred_element_type=jnp.float32
    )
    return (which, term)


def add_term(total, which, term):
    current = lax.dynamic_index_in_dim(total, which, 0, keepdims=False)
    return lax.dynamic_update_index_in_dim(total, current + term, which, 0)


def body(pair_blocks, block_list, block_count, coef):
    coef_rows = lax.all_gather(coef, "pq", axis=0, tiled=True)
    coef_full = lax.all_gather(coef_rows, "grp", axis=1, tiled=True)
    panels = pair_blocks.shape[0]
    tile = pair_blocks.shape[2]
    nblk = coef_full.shape[0] // tile
    width = coef_full.shape[1]
    empty = jnp.zeros((KL_PANEL, width, width), jnp.float32)
    size_pq = lax.axis_size("pq")
    bit = size_pq.bit_length() - 2
    other_blocks, other_list, other_count = partner(
        (pair_blocks, block_list, block_count), "pq", bit
    )
    upper = lax.axis_index("pq") // (size_pq // 2) % 2
    stacked_blocks = jnp.stack([pair_blocks, other_blocks])
    stacked_list = jnp.stack([block_list, other_list])
    pieces = []
    for panel in range(panels):
        own_count = block_count[panel, 0]
        far_count = other_count[panel, 0]
        first_count = jnp.where(upper == 1, far_count, own_count)
        combined = own_count + far_count
        middle = (combined + 1) // 2
        lower_bound = jnp.where(upper == 1, middle, 0)
        upper_bound = jnp.where(upper == 1, combined, middle)

        def step(slot, total):
            source = jnp.where(slot < first_count, upper, 1 - upper)
            place = jnp.where(slot < first_count, slot, slot - first_count)
            block = stacked_blocks[source, panel, place]
            ident = stacked_list[source, panel, place]
            which, term = block_term(block, ident, coef_full, tile, nblk)
            return add_term(total, which, term)

        totals = lax.fori_loop(lower_bound, upper_bound, step, empty)
        pieces.append(totals)
    joined = jnp.concatenate(pieces, 0)
    return lax.psum_scatter(joined, "pq", scatter_dimension=1, tiled=True)


def solution(mesh):
    in_specs = (P("grp", "pq", None, None), P("grp", "pq"), P("grp", "pq"), P("pq", "grp"))
    out_specs = P("grp", "pq", None)
    return jax.shard_map(body, mesh=mesh, in_specs=in_specs, out_specs=out_specs, check_vma=False)
```

profile of v0, /device:TPU:0, one launch (start us, length us, event | category | flops | bytes accessed | tf_op | source)
XLA Modules:
  0.0 368.6 jit_solution(15442970876502260729)
XLA Ops:
  7.3 46.4 %all-gather.3.cloned.1.call-done = bf16[4096,256]{1,0:T(8,128)(2,1)} async-done(((bf16[256,256]{1,0:T(8,128)(2,1)}), bf16[4096,256]{1,0:T(8,128)(2,1)}) %all-gather.3.cloned.1.call-update) | async-done | bytes 2097168 | tf_op jit(solution)/shard_map/all_gather | solution.py:35
  54.5 2.3 collective-permute-start
  58.8 49.5 %collective-permute-done = s32[2,1]{0,1:T(1,128)S(1)} collective-permute-done((s32[2,1]{0,1:T(1,128)}, s32[2,1]{0,1:T(1,128)S(1)}, u32[]{:S(2)}, u32[]{:S(2)}) %collective-permute-start) | collective-permute-done | bytes 40 | tf_op jit(solution)/shard_map/ppermute | solution.py:12
  113.7 1.7 pad_maximum_fusion.1
  115.4 1.7 broadcast_in_dim.18.clone
  117.0 62.6 %while.27 = (s32[]{:T(128)}, f32[2,512,512]{2,1,0:T(8,128)}, s32[]{:T(128)}, s32[]{:T(128)}, s32[]{:T(128)}, /*index=5*/s32[]{:T(128)}, s32[2,2,18]{2,1,0:T(2,12...) while((s32[]{:T(128)}, f32[2,512,512]{2,1,0:T(8,128)}, ...), condition=%wide.region_3.4_spmd, body=%wide.region_2.3_spmd.sunk | while | flops 84213824 | bytes 4490093 | solution.py:68
  121.5 2.4 fusion.41
  128.4 2.4 fusion.41
  135.3 2.5 fusion.41
  142.4 2.4 fusion.41
  149.3 2.4 fusion.41
  156.2 2.4 fusion.41
  163.1 2.5 fusion.41
  170.1 2.5 fusion.41
  177.1 2.5 fusion.41
  179.9 62.1 %while.26 = (s32[]{:T(128)}, f32[2,512,512]{2,1,0:T(8,128)S(1)}, s32[]{:T(128)}, s32[]{:T(128)}, s32[]{:T(128)}, /*index=5*/s32[]{:T(128)}, s32[2,2,18]{2,1,0:T(...) while((s32[]{:T(128)}, f32[2,512,512]{2,1,0:T(8,128)S(1)}, ...), condition=%wide.region_1.2_spmd, body=%wide.region_0.1_spmd.sunk | while | flops 84213824 | bytes 4490093 | solution.py:68
  183.2 1.4 fusion.37
  188.0 1.4 fusion.37
  192.8 1.4 fusion.37
  207.1 1.4 fusion.37
  211.9 1.4 fusion.37
  216.6 1.4 fusion.37
  242.0 4.2 %pad_maximum_fusion = f32[4,512,512]{2,1,0:T(8,128)} fusion(f32[2,512,512]{2,1,0:T(8,128)} %get-tuple-element.300, f32[2,512,512]{2,1,0:T(8,128)S(1)} %get-tuple-element.299), kind=kLoop, calls=%fused_computation.23 | loop fusion | flops 1048576 | bytes 8388608 | tf_op jit(solution)/shard_map/concatenate | solution.py:70
  246.2 115.8 %reduce-scatter.2.cloned.1.call-done = f32[4,32,512]{2,1,0:T(8,128)} async-done(((f32[4,512,512]{2,1,0:T(8,128)}), f32[4,32,512]{2,1,0:T(8,128)}) %reduce-scatter.2.cloned.1.call-update) | async-done | bytes 262160 | tf_op jit(solution)/shard_map/reduce_scatter | solution.py:71
  (70 shorter events, 40.4 us)
Async XLA Ops:
  6.5 107.2 %copy-start = (bf16[2,18,128,128]{3,2,1,0:T(8,128)(2,1)S(1)}, bf16[2,18,128,128]{3,2,1,0:T(8,128)(2,1)}, u32[]{:S(2)}) copy-start(bf16[2,18,128,128]{3,2,1,0:T(8,128)(2,1)} %param.8) | copy-start | bytes 3538948
  6.5 107.1 %copy-start.1 = (s32[2,18]{1,0:T(2,128)S(1)}, s32[2,18]{1,0:T(2,128)}, u32[]{:S(2)}) copy-start(s32[2,18]{1,0:T(2,128)} %param.9) | copy-start | bytes 436
  6.5 47.2 %all-gather.3.cloned.1.call-start = ((), (), s32[]{:S(2)}) async-start(), calls=%async_computation.1 | async-start | bytes 2228224 | tf_op jit(solution)/shard_map/all_gather | solution.py:35
  7.3 108.1 %all-gather.5.cloned.1.call-start = ((), (), s32[]{:S(2)}) async-start(), calls=%async_computation.2 | async-start | bytes 6291456 | tf_op jit(solution)/shard_map/all_gather | solution.py:36
  53.7 308.3 %reduce-scatter.2.cloned.1.call-start = ((), (), s32[]{:S(2)}) async-start(), calls=%async_computation.3 | async-start | bytes 4456448 | tf_op jit(solution)/shard_map/reduce_scatter | solution.py:71
  53.8 59.9 %collective-permute-start.2 = (bf16[2,18,128,128]{3,2,1,0:T(8,128)(2,1)}, bf16[2,18,128,128]{3,2,1,0:T(8,128)(2,1)S(1)}, u32[]{:S(2)}, u32[]{:S(2)}) collective-permute-start(bf16[2,18,128,128]{3,2,1,0:T(8,128)(2,1)} %param.8), channel_id=1, source_target_pairs={{0,8},{1,9},{2,10},{3,11},{4,12},{5,13},{6,14},{7,15},{8,0},{9,1},... | collective-permute-start | bytes 3538952 | tf_op jit(solution)/shard_map/ppermute | solution.py:12
  54.5 53.8 %collective-permute-start = (s32[2,1]{0,1:T(1,128)}, s32[2,1]{0,1:T(1,128)S(1)}, u32[]{:S(2)}, u32[]{:S(2)}) collective-permute-start(s32[2,1]{0,1:T(1,128)} %param.10), channel_id=1, source_target_pairs={{0,8},{1,9},{2,10},{3,11},{4,12},{5,13},{6,14},{7,15},{8,0},{9,1},... | collective-permute-start | bytes 32 | tf_op jit(solution)/shard_map/ppermute | solution.py:12
  56.8 56.9 %collective-permute-start.1 = (s32[2,18]{1,0:T(2,128)}, s32[2,18]{1,0:T(2,128)S(1)}, u32[]{:S(2)}, u32[]{:S(2)}) collective-permute-start(s32[2,18]{1,0:T(2,128)} %param.9), channel_id=1, source_target_pairs={{0,8},{1,9},{2,10},{3,11},{4,12},{5,13},{6,14},{7,15},{8,0},{9,1},... | collective-permute-start | bytes 440 | tf_op jit(solution)/shard_map/ppermute | solution.py:12
Sparse Core Ops, SparseCore 0:
  9.5 44.1 all-gather.2
  55.2 55.3 all-gather.4
  246.3 115.6 reduce-scatter.1
where the time goes:
time: 373 us; the launch traced here: 369 us
  waiting for transfers between devices  212 us (57%)
  loops' own time  57.9 us (16%)
  matrix products  40.7 us (11%)
  local copies, waits for them, and re-layouts  29.9 us (8%)
  between operations  18 us (5%)
  other arithmetic  5.86 us (2%)
    reduce_scatter x1, waiting for transfers between devices, body(): return lax.psum_scatter(joined, 'pq', scatter_dimension=1, tiled=True)  116 us
    another operation x2, loops' own time, body(): totals = lax.fori_loop(lower_bound, upper_bound, step, empty)  57.9 us
    ppermute x3, waiting for transfers between devices, partner(): return lax.ppermute(value, axis, pairs)  49.5 us
    all_gather x1, waiting for transfers between devices, body(): coef_rows = lax.all_gather(coef, 'pq', axis=0, tiled=True)  46.4 us
    dot_general x22, matrix products, block_term(): lax.dot_general(row_coef, half, (((0,), (0,)), ((), ())), preferred_eleme...  40.7 us
    dynamic_slice x22, local copies, waits for them, and re-layouts, step(): ident = stacked_list[source, panel, place]  13.4 us
    dynamic_slice x22, local copies, waits for them, and re-layouts, add_term(): current = lax.dynamic_index_in_dim(total, which, 0, keepdims=False)  12.7 us
  transfers between devices with their start and end apart: 6, of which 3 were waited for; matrix products, arithmetic and copies ran while one was open for 1% of the time, Pallas kernels for 0%

commit v1 on v0

v1 whole, which is shorter than its diff:
```python
import functools

import jax
import jax.numpy as jnp
from jax import lax
from jax.experimental import pallas as pl
from jax.experimental.pallas import tpu as pltpu
from jax.sharding import PartitionSpec as P

KL_PANEL = 2
MESH = pl.DeviceIdType.MESH
DIRECT_LIMIT = 64
UNROLL = 3


def coords(mine, n_z):
    core, yy, zz = lax.rem(mine, 2), lax.rem(lax.div(mine, 2), 2), lax.div(mine, 4)
    return core, yy, zz, lambda step: lax.rem(zz + step, n_z)


def pq_of(z, y, c):
    return z * 4 + y * 2 + c


def meet(peers):
    barrier = pltpu.get_barrier_semaphore()
    for peer in peers:
        pl.semaphore_signal(barrier, inc=1, device_id=peer, device_id_type=MESH)
    pl.semaphore_wait(barrier, len(peers))


def gather_kernel(n_grp, n_pq, tile, coef_ref, full, flipped, send_sem, recv_sem):
    rows, cols = coef_ref.shape
    n_z = n_pq // 4
    mine_g, mine = lax.axis_index("grp"), lax.axis_index("pq")
    core, yy, zz, z_at = coords(mine, n_z)
    core_peer = (mine_g, pq_of(zz, yy, 1 - core))
    y_peer = (mine_g, pq_of(zz, 1 - yy, core))
    x_peer = (1 - mine_g, mine)
    z_peers = [(mine_g, pq_of(z_at(s), yy, core)) for s in range(1, n_z)]
    meet([core_peer, y_peer, x_peer] + z_peers)

    first_g = lax.rem(mine_g + 1 - core, 2)
    first_y = lax.rem(yy + core, 2)
    second_g = lax.rem(mine_g + core, 2)
    second_y = lax.rem(yy + 1 - core, 2)
    first_peer = (first_g, pq_of(zz, first_y, core))
    second_peer = (second_g, pq_of(zz, second_y, core))
    started = []

    def place(g, p):
        return full.at[g, pl.ds(pl.multiple_of(p * rows, rows), rows), :]

    def send(src, g, p, peer):
        copy = pltpu.make_async_remote_copy(
            src_ref=src, dst_ref=place(g, p), send_sem=send_sem.at[len(started)],
            recv_sem=recv_sem.at[g, p], device_id=peer, device_id_type=MESH,
        )
        copy.start()
        started.append(copy)

    def flip(src, g, p):
        turned = src[...].T
        for k in range(rows // tile):
            flipped[p * (rows // tile) + k, pl.ds(pl.multiple_of(g * cols, cols), cols), :] = (
                turned[:, k * tile:(k + 1) * tile]
            )

    def relay(g, p, targets):
        pltpu.make_async_copy(place(g, p), place(g, p), recv_sem.at[g, p]).wait()
        for peer in targets:
            send(place(g, p), g, p, peer)
        flip(place(g, p), g, p)

    for peer in [first_peer, second_peer] + z_peers + [core_peer]:
        send(coef_ref, mine_g, mine, peer)
    full[mine_g, pl.ds(pl.multiple_of(mine * rows, rows), rows), :] = coef_ref[...]
    flip(coef_ref, mine_g, mine)
    order = [1, n_z - 1] + list(range(2, n_z - 1))
    relay(first_g, pq_of(zz, first_y, core), [second_peer, core_peer])
    for step in order:
        relay(mine_g, pq_of(z_at(step), yy, core), [first_peer, second_peer, core_peer])
    for step in order:
        relay(first_g, pq_of(z_at(step), first_y, core), [second_peer, core_peer])
    for step in [0] + order:
        relay(second_g, pq_of(z_at(step), second_y, core), [core_peer])
    for step in [0] + order:
        relay(1 - mine_g, pq_of(z_at(step), 1 - yy, core), [core_peer])
    for g, y in ((mine_g, yy), (1 - mine_g, yy), (mine_g, 1 - yy), (1 - mine_g, 1 - yy)):
        for step in [0] + order:
            relay(g, pq_of(z_at(step), y, 1 - core), [])
    for copy in started:
        copy.wait_send()


def transform_kernel(
    n_grp, n_pq, blocks_ref, list_ref, count_ref, full, flipped,
    own_ref, other_ref, rows_p, halves, acc,
):
    panels, slots, tile = blocks_ref.shape[0], blocks_ref.shape[1], blocks_ref.shape[2]
    nblk, width = flipped.shape[0], flipped.shape[1]
    cols, chunk, n_z = width // n_grp, width // n_pq, n_pq // 4
    core = lax.rem(lax.axis_index("pq"), 2)
    pair = 2 * tile

    for panel in range(panels):
        count = count_ref[panel, 0]

        def step(turn, used):
            for k in range(UNROLL):
                slot = turn * UNROLL + k
                live = slot < count
                slot = jnp.minimum(slot, slots - 1)
                ident = list_ref[panel, slot]
                which = jnp.where(live, lax.div(ident, nblk * nblk), KL_PANEL)
                row_blk = lax.rem(lax.div(ident, nblk), nblk)
                col_blk = lax.rem(ident, nblk)
                spot = jnp.where(which == 0, used[0], jnp.where(which == 1, used[1], 0))
                used = tuple(u + jnp.where(which == kl, 1, 0) for kl, u in enumerate(used))
                at = pl.ds(pl.multiple_of(spot * tile, tile), tile)
                rows_p[which, :, at] = flipped[row_blk]
                for g in range(n_grp):
                    coefs = full[g, pl.ds(pl.multiple_of(col_blk * tile, tile), tile), :]
                    half = jnp.dot(blocks_ref[panel, slot], coefs, preferred_element_type=jnp.float32)
                    halves[which, at, g * cols:(g + 1) * cols] = half.astype(jnp.bfloat16)
            return used

        zero = jnp.int32(0)
        used = lax.fori_loop(0, lax.div(count + UNROLL - 1, UNROLL), step, (zero,) * KL_PANEL)
        for kl in range(KL_PANEL):
            at = pl.ds(pl.multiple_of(used[kl] * tile, tile), tile)
            rows_p[kl, :, at] = jnp.zeros((width, tile), jnp.bfloat16)
            halves[kl, at, :] = jnp.zeros((tile, width), jnp.bfloat16)
            acc[...] = jnp.zeros_like(acc)

            def add(turn, carry):
                at = pl.ds(pl.multiple_of(turn * pair, pair), pair)
                acc[...] += jnp.dot(
                    rows_p[kl, :, at], halves[kl, at, :], preferred_element_type=jnp.float32
                )
                return carry

            lax.fori_loop(0, lax.div(used[kl] + 1, 2), add, 0)
            for y in range(2):
                for z in range(n_z):
                    for c, ref in ((core, own_ref), (1 - core, other_ref)):
                        at = pl.multiple_of((z * 4 + y * 2 + c) * chunk, chunk)
                        ref[panel, y, z, kl] = acc[pl.ds(at, chunk), :].astype(ref.dtype)


def scatter_kernel(
    own, other, out_ref, sum_bf, fin_bf, from_core, from_y, from_z,
    send_sem, core_recv, y_recv, z_recv,
):
    panels, n_z = own.shape[0], own.shape[2]
    f32, bf16 = jnp.float32, jnp.bfloat16
    mine_g, mine = lax.axis_index("grp"), lax.axis_index("pq")
    core, yy, zz, z_at = coords(mine, n_z)
    core_peer = (mine_g, pq_of(zz, yy, 1 - core))
    y_peer = (mine_g, pq_of(zz, 1 - yy, core))
    z_peers = [(mine_g, pq_of(z_at(s), yy, core)) for s in range(1, n_z)]
    meet([core_peer, y_peer] + z_peers)
    sent = []

    def push(src, dst, recv, peer):
        copy = pltpu.make_async_remote_copy(
            src_ref=src, dst_ref=dst, send_sem=send_sem.at[len(sent)],
            recv_sem=recv, device_id=peer, device_id_type=MESH,
        )
        copy.start()
        sent.append(copy)

    def landed(dst, recv):
        pltpu.make_async_copy(dst, dst, recv).wait()

    far_first = list(range(1, n_z)) + [0]
    for y in (1 - yy, yy):
        for panel in range(panels):
            push(other.at[panel, y], from_core.at[panel, y], core_recv.at[panel, y], core_peer)
    for panel in range(panels):
        landed(from_core.at[panel, 1 - yy], core_recv.at[panel, 1 - yy])
    for s in far_first:
        z = z_at(s)
        for panel in range(panels):
            total = own[panel, 1 - yy, z] + from_core[panel, 1 - yy, z].astype(f32)
            sum_bf[panel, s] = total.astype(bf16)
            push(sum_bf.at[panel, s], from_y.at[panel, s], y_recv.at[panel, s], y_peer)
    for panel in range(panels):
        landed(from_core.at[panel, yy], core_recv.at[panel, yy])
    for s in far_first:
        z = z_at(s)
        for panel in range(panels):
            landed(from_y.at[panel, s], y_recv.at[panel, s])
            total = (
                own[panel, yy, z] + from_core[panel, yy, z].astype(f32)
                + from_y[panel, s].astype(f32)
            )
            if s:
                fin_bf[panel, s] = total.astype(bf16)
                push(fin_bf.at[panel, s], from_z.at[panel, s], z_recv.at[panel, s], z_peers[s - 1])
            else:
                out_ref[pl.ds(panel * KL_PANEL, KL_PANEL)] = total
    for panel in range(panels):
        total = out_ref[pl.ds(panel * KL_PANEL, KL_PANEL)]
        for s in range(1, n_z):
            landed(from_z.at[panel, s], z_recv.at[panel, s])
            total += from_z[panel, s].astype(f32)
        out_ref[pl.ds(panel * KL_PANEL, KL_PANEL)] = total
    for copy in sent:
        copy.wait_send()


def direct(n_grp, n_pq, pair_blocks, block_list, block_count, coef):
    panels, slots, tile, _ = pair_blocks.shape
    rows, cols = coef.shape
    width, nao, n_z = n_grp * cols, n_pq * rows, n_pq // 4
    chunk = width // n_pq
    bf16, f32 = jnp.bfloat16, jnp.float32
    vmem = pl.BlockSpec(memory_space=pltpu.VMEM)
    smem = pl.BlockSpec(memory_space=pltpu.SMEM)
    sems = pltpu.SemaphoreType.DMA
    shape = jax.ShapeDtypeStruct
    mib = 2**20
    n_gather = 2 + n_z + 3 * (n_z - 1) + 2 * n_z + 2 * n_z
    full, flipped = pl.pallas_call(
        functools.partial(gather_kernel, n_grp, n_pq, tile),
        out_shape=(shape((n_grp, nao, cols), bf16), shape((nao // tile, width, tile), bf16)),
        in_specs=[vmem],
        out_specs=(vmem, vmem),
        scratch_shapes=[sems((n_gather,)), sems((n_grp, n_pq))],
        compiler_params=pltpu.CompilerParams(
            collective_id=0, has_side_effects=True, vmem_limit_bytes=24 * mib
        ),
    )(coef)
    padded = slots + 1 + slots % 2
    part = (panels, 2, n_z, KL_PANEL, chunk, width)
    own, other = pl.pallas_call(
        functools.partial(transform_kernel, n_grp, n_pq),
        out_shape=(shape(part, f32), shape(part, bf16)),
        in_specs=[vmem, smem, smem, vmem, vmem],
        out_specs=(vmem, vmem),
        scratch_shapes=[
            pltpu.VMEM((KL_PANEL + 1, width, padded * tile), bf16),
            pltpu.VMEM((KL_PANEL + 1, padded * tile, width), bf16),
            pltpu.VMEM((width, width), f32),
        ],
        compiler_params=pltpu.CompilerParams(vmem_limit_bytes=40 * mib),
    )(pair_blocks, block_list, block_count, full, flipped)
    pieces = (panels, n_z, KL_PANEL, chunk, width)
    return pl.pallas_call(
        scatter_kernel,
        out_shape=shape((panels * KL_PANEL, chunk, width), f32),
        in_specs=[vmem, vmem],
        out_specs=vmem,
        scratch_shapes=[
            pltpu.VMEM(pieces, bf16),
            pltpu.VMEM(pieces, bf16),
            pltpu.VMEM(part, bf16),
            pltpu.VMEM(pieces, bf16),
            pltpu.VMEM(pieces, bf16),
            sems((panels * (1 + 2 * n_z) + panels,)),
            sems((panels, 2)),
            sems((panels, n_z)),
            sems((panels, n_z)),
        ],
        compiler_params=pltpu.CompilerParams(
            collective_id=1, has_side_effects=True, vmem_limit_bytes=24 * mib
        ),
    )(own, other)


def local_kernel(nblk, blocks_ref, list_ref, count_ref, coef_ref, out_ref):
    panels, slots, tile = blocks_ref.shape[0], blocks_ref.shape[1], blocks_ref.shape[2]
    out_ref[...] = jnp.zeros_like(out_ref)
    for panel in range(panels):

        def step(slot, carry):
            ident = list_ref[panel, slot]
            which = panel * KL_PANEL + lax.div(ident, nblk * nblk)
            row_blk = lax.rem(lax.div(ident, nblk), nblk)
            col_blk = lax.rem(ident, nblk)
            col_coef = coef_ref[pl.ds(pl.multiple_of(col_blk * tile, tile), tile), :]
            row_coef = coef_ref[pl.ds(pl.multiple_of(row_blk * tile, tile), tile), :]
            half = jnp.dot(blocks_ref[panel, slot], col_coef, preferred_element_type=jnp.float32)
            out_ref[which] += lax.dot_general(
                row_coef, half.astype(jnp.bfloat16), (((0,), (0,)), ((), ())),
                preferred_element_type=jnp.float32,
            )
            return carry

        lax.fori_loop(0, count_ref[panel, 0], step, 0)


def gathered(pair_blocks, block_list, block_count, coef):
    coef_rows = lax.all_gather(coef, "pq", axis=0, tiled=True)
    coef_full = lax.all_gather(coef_rows, "grp", axis=1, tiled=True)
    nao, width = coef_full.shape
    vmem = pl.BlockSpec(memory_space=pltpu.VMEM)
    smem = pl.BlockSpec(memory_space=pltpu.SMEM)
    joined = pl.pallas_call(
        functools.partial(local_kernel, nao // pair_blocks.shape[2]),
        out_shape=jax.ShapeDtypeStruct((pair_blocks.shape[0] * KL_PANEL, width, width), jnp.float32),
        in_specs=[vmem, smem, smem, vmem],
        out_specs=vmem,
        compiler_params=pltpu.CompilerParams(vmem_limit_bytes=48 * 2**20),
    )(pair_blocks, block_list, block_count, coef_full)
    return lax.psum_scatter(joined, "pq", scatter_dimension=1, tiled=True)


def body(pair_blocks, block_list, block_count, coef):
    n_grp, n_pq = lax.axis_size("grp"), lax.axis_size("pq")
    rows, cols = coef.shape
    tile = pair_blocks.shape[2]
    fits = n_grp == 2 and n_pq % 8 == 0 and n_grp * n_pq <= DIRECT_LIMIT
    if fits and rows % tile == 0 and cols % 128 == 0:
        return direct(n_grp, n_pq, pair_blocks, block_list, block_count, coef)
    return gathered(pair_blocks, block_list, block_count, coef)


def solution(mesh):
    in_specs = (P("grp", "pq", None, None), P("grp", "pq"), P("grp", "pq"), P("pq", "grp"))
    out_specs = P("grp", "pq", None)
    return jax.shard_map(body, mesh=mesh, in_specs=in_specs, out_specs=out_specs, check_vma=False)
```

time: 373 us -> 66 us (0.18); the launches traced: 369 us -> 65.6 us
  waiting for transfers between devices: 212 us -> 0 us
  Pallas kernels: 0 us -> 61.2 us
  loops' own time: 57.9 us -> 0 us
  matrix products: 40.7 us -> 0 us
  local copies, waits for them, and re-layouts: 29.9 us -> 4.29 us
  between operations: 18 us -> 0.04 us
  other arithmetic: 5.86 us -> 0 us
    reduce_scatter x1 -> x0, waiting for transfers between devices: 116 us -> none  [body(): return lax.psum_scatter(joined, 'pq', scatter_dimension=1, tiled=True)]
    pallas_call x0 -> x3, Pallas kernels: none -> 61.2 us  [the longest x1 30.8 us: direct(): pl.pallas_call(functools.partial(gather_kernel, n_grp, n_pq, tile), out_s...]
    another operation x2 -> x0, loops' own time: 57.9 us -> none  [body(): totals = lax.fori_loop(lower_bound, upper_bound, step, empty)]
    ppermute x3 -> x0, waiting for transfers between devices: 49.5 us -> none  [partner(): return lax.ppermute(value, axis, pairs)]
    all_gather x2 -> x0, waiting for transfers between devices: 46.4 us -> none  [the longest x1 46.4 us: body(): coef_rows = lax.all_gather(coef, 'pq', axis=0, tiled=True)]
    dot_general x22 -> x0, matrix products: 40.7 us -> none  [block_term(): lax.dot_general(row_coef, half, (((0,), (0,)), ((), ())), preferred_eleme...]
    dynamic_slice x44 -> x0, local copies, waits for them, and re-layouts: 26 us -> none  [the longest x22 13.4 us: step(): ident = stacked_list[source, panel, place]]
    unnamed x4 -> x8, local copies, waits for them, and re-layouts: 0.01 us -> 4.29 us
  transfers between devices with their start and end apart: 6 -> 0, of which waited for: 3 -> 0; matrix products, arithmetic and copies ran while one was open for 1% -> 0% of each run, Pallas kernels for 0% -> 0%
where the time goes in v1:
time: 66 us; the launch traced here: 65.6 us
  Pallas kernels  61.2 us (93%)
  local copies, waits for them, and re-layouts  4.29 us (6%)
    pallas_call x1, Pallas kernels, direct(): pl.pallas_call(functools.partial(gather_kernel, n_grp, n_pq, tile), out_s...  30.8 us
    pallas_call x1, Pallas kernels, direct(): pl.pallas_call(scatter_kernel, out_shape=shape((panels * KL_PANEL, chunk,...  23.7 us
    pallas_call x1, Pallas kernels, direct(): pl.pallas_call(functools.partial(transform_kernel, n_grp, n_pq), out_shap...  6.74 us
    unnamed x8, local copies, waits for them, and re-layouts  4.29 us

profile of v1, /device:TPU:0, one launch (start us, length us, event | category | flops | bytes accessed | tf_op | source)
XLA Modules:
  0.0 65.6 jit_solution(15507922219030619299)
XLA Ops:
  0.0 0.7 %copy.5.count_ref = s32[2,1]{1,0:T(2,128)S(1)} copy(s32[2,1]{0,1:T(1,128)} %param.6) | data formatting | bytes 16 | tf_op args[2]
  0.7 0.0 copy-start.1
  0.7 0.9 %copy-done.1 = bf16[256,256]{1,0:T(8,128)(2,1)S(1)} copy-done((bf16[256,256]{1,0:T(8,128)(2,1)S(1)}, bf16[256,256]{1,0:T(8,128)(2,1)}, u32[]{:S(2)}) %copy-start.1) | copy-done | bytes 131096
  1.6 30.8 %shard_map.46 = (bf16[2,4096,256]{2,1,0:T(8,128)(2,1)S(1)}, bf16[32,512,128]{2,1,0:T(8,128)(2,1)S(1)}) custom-call(bf16[256,256]{1,0:T(8,128)(2,1)S(1)} %copy-done.1), custom_call_target="tpu_custom_call" | custom-call | tf_op jit(solution)/shard_map/pallas_call | solution.py:225
  32.5 0.0 copy-start
  32.5 1.3 %copy-done = bf16[2,18,128,128]{3,2,1,0:T(8,128)(2,1)S(1)} copy-done((bf16[2,18,128,128]{3,2,1,0:T(8,128)(2,1)S(1)}, bf16[2,18,128,128]{3,2,1,0:T(8,128)(2,1)}, u32[]{:S(2)}) %copy-start) | copy-done | bytes 1179672
  33.7 0.0 copy-start.2
  33.7 0.7 %copy-done.2 = s32[2,18]{1,0:T(2,128)S(1)} copy-done((s32[2,18]{1,0:T(2,128)S(1)}, s32[2,18]{1,0:T(2,128)}, u32[]{:S(2)}) %copy-start.2) | copy-done | bytes 168
  34.4 6.7 %shard_map.47 = (f32[2,2,4,2,32,512]{5,4,3,2,1,0:T(8,128)S(1)}, bf16[2,2,4,2,32,512]{5,4,3,2,1,0:T(8,128)(2,1)S(1)}) custom-call(bf16[2,18,128,128]{3,2,1,0:T(8,128)(2,1)S(1)} %copy-done, s32[2,18]{1,0:T(2,128)S(1)} %copy-done.2, s32[2,1]{1,0:T(2,128)S(1)} %copy.5.count_ref, bf16[2,4096,256]{2,1,0:T(8,128)(2,1)S(1)} %get-tuple-element.9.full, ...), custom_call_target="tpu_custom_call" | custom-call | tf_op jit(solution)/shard_map/pallas_call | solution.py:237
  41.2 23.7 %shard_map.48 = f32[4,32,512]{2,1,0:T(8,128)S(1)} custom-call(f32[2,2,4,2,32,512]{5,4,3,2,1,0:T(8,128)S(1)} %get-tuple-element.11.own, bf16[2,2,4,2,32,512]{5,4,3,2,1,0:T(8,128)(2,1)S(1)} %get-tuple-element.12.other), custom_call_target="tpu_custom_call" | custom-call | tf_op jit(solution)/shard_map/pallas_call | solution.py:250
  64.9 0.7 %copy.7 = f32[4,32,512]{2,1,0:T(8,128)} copy(f32[4,32,512]{2,1,0:T(8,128)S(1)} %shard_map.48) | data formatting | bytes 524288
Async XLA Ops:
  0.7 0.9 %copy-start.1 = (bf16[256,256]{1,0:T(8,128)(2,1)S(1)}, bf16[256,256]{1,0:T(8,128)(2,1)}, u32[]{:S(2)}) copy-start(bf16[256,256]{1,0:T(8,128)(2,1)} %coef_ref.1) | copy-start | bytes 393220
  32.5 1.3 %copy-start = (bf16[2,18,128,128]{3,2,1,0:T(8,128)(2,1)S(1)}, bf16[2,18,128,128]{3,2,1,0:T(8,128)(2,1)}, u32[]{:S(2)}) copy-start(bf16[2,18,128,128]{3,2,1,0:T(8,128)(2,1)} %blocks_ref.1) | copy-start | bytes 3538948
  33.7 0.7 %copy-start.2 = (s32[2,18]{1,0:T(2,128)S(1)}, s32[2,18]{1,0:T(2,128)}, u32[]{:S(2)}) copy-start(s32[2,18]{1,0:T(2,128)} %list_ref.1) | copy-start | bytes 436

commit v2 on v1

--- a/solution.py
+++ b/solution.py
@@ -9,13 +9,18 @@
 
 KL_PANEL = 2
 MESH = pl.DeviceIdType.MESH
-DIRECT_LIMIT = 64
 UNROLL = 3
 
 
-def coords(mine, n_z):
+LINE = 4
+
+
+def coords(mine):
     core, yy, zz = lax.rem(mine, 2), lax.rem(lax.div(mine, 2), 2), lax.div(mine, 4)
-    return core, yy, zz, lambda step: lax.rem(zz + step, n_z)
+    half = lax.div(zz, 2)
+    beside = 2 * half + 1 - lax.rem(zz, 2)
+    across = 3 - zz
+    return core, yy, zz, (beside, 2 - half, 3 - 3 * half), across
 
 
 def pq_of(z, y, c):
@@ -29,68 +34,103 @@
     pl.semaphore_wait(barrier, len(peers))
 
 
-def gather_kernel(n_grp, n_pq, tile, coef_ref, full, flipped, send_sem, recv_sem):
+def gather_kernel(n_grp, n_pq, tile, coef_ref, full, flipped, send_sem, recv_sem, load_sem):
     rows, cols = coef_ref.shape
-    n_z = n_pq // 4
+    subs = rows // tile
     mine_g, mine = lax.axis_index("grp"), lax.axis_index("pq")
-    core, yy, zz, z_at = coords(mine, n_z)
+    core, yy, zz, nearest, across = coords(mine)
+    middle = (zz > 0) & (zz < LINE - 1)
     core_peer = (mine_g, pq_of(zz, yy, 1 - core))
     y_peer = (mine_g, pq_of(zz, 1 - yy, core))
     x_peer = (1 - mine_g, mine)
-    z_peers = [(mine_g, pq_of(z_at(s), yy, core)) for s in range(1, n_z)]
-    meet([core_peer, y_peer, x_peer] + z_peers)
-
-    first_g = lax.rem(mine_g + 1 - core, 2)
-    first_y = lax.rem(yy + core, 2)
-    second_g = lax.rem(mine_g + core, 2)
-    second_y = lax.rem(yy + 1 - core, 2)
+    beside_peer = (mine_g, pq_of(nearest[0], yy, core))
+    across_peer = (mine_g, pq_of(across, yy, core))
+
+    def place(g, p, k):
+        at = pl.multiple_of(p * rows + k * tile, tile)
+        return full.at[g, pl.ds(at, tile), :]
+
+    own_rows = full.at[mine_g, pl.ds(pl.multiple_of(mine * rows, rows), rows), :]
+    load = pltpu.make_async_copy(coef_ref, own_rows, load_sem)
+    load.start()
+    meet([core_peer, y_peer, x_peer, beside_peer, across_peer])
+    load.wait()
+
+    first_g, first_y = lax.rem(mine_g + 1 - core, 2), lax.rem(yy + core, 2)
+    second_g, second_y = lax.rem(mine_g + core, 2), lax.rem(yy + 1 - core, 2)
     first_peer = (first_g, pq_of(zz, first_y, core))
     second_peer = (second_g, pq_of(zz, second_y, core))
     started = []
 
-    def place(g, p):
-        return full.at[g, pl.ds(pl.multiple_of(p * rows, rows), rows), :]
-
-    def send(src, g, p, peer):
+    def send(g, p, k, peer, only=None):
         copy = pltpu.make_async_remote_copy(
-            src_ref=src, dst_ref=place(g, p), send_sem=send_sem.at[len(started)],
-            recv_sem=recv_sem.at[g, p], device_id=peer, device_id_type=MESH,
+            src_ref=place(g, p, k), dst_ref=place(g, p, k), send_sem=send_sem.at[len(started)],
+            recv_sem=recv_sem.at[g, p, k], device_id=peer, device_id_type=MESH,
         )
-        copy.start()
-        started.append(copy)
-
-    def flip(src, g, p):
-        turned = src[...].T
-        for k in range(rows // tile):
-            flipped[p * (rows // tile) + k, pl.ds(pl.multiple_of(g * cols, cols), cols), :] = (
-                turned[:, k * tile:(k + 1) * tile]
-            )
-
-    def relay(g, p, targets):
-        pltpu.make_async_copy(place(g, p), place(g, p), recv_sem.at[g, p]).wait()
-        for peer in targets:
-            send(place(g, p), g, p, peer)
-        flip(place(g, p), g, p)
-
-    for peer in [first_peer, second_peer] + z_peers + [core_peer]:
-        send(coef_ref, mine_g, mine, peer)
-    full[mine_g, pl.ds(pl.multiple_of(mine * rows, rows), rows), :] = coef_ref[...]
-    flip(coef_ref, mine_g, mine)
-    order = [1, n_z - 1] + list(range(2, n_z - 1))
-    relay(first_g, pq_of(zz, first_y, core), [second_peer, core_peer])
-    for step in order:
-        relay(mine_g, pq_of(z_at(step), yy, core), [first_peer, second_peer, core_peer])
-    for step in order:
-        relay(first_g, pq_of(z_at(step), first_y, core), [second_peer, core_peer])
-    for step in [0] + order:
-        relay(second_g, pq_of(z_at(step), second_y, core), [core_peer])
-    for step in [0] + order:
-        relay(1 - mine_g, pq_of(z_at(step), 1 - yy, core), [core_peer])
-    for g, y in ((mine_g, yy), (1 - mine_g, yy), (mine_g, 1 - yy), (1 - mine_g, 1 - yy)):
-        for step in [0] + order:
-            relay(g, pq_of(z_at(step), y, 1 - core), [])
-    for copy in started:
-        copy.wait_send()
+        if only is None:
+            copy.start()
+        else:
+            pl.when(only)(copy.start)
+        started.append((copy, only))
+
+    def flip(g, p, k):
+        at = pl.multiple_of(g * cols, cols)
+        flipped[p * subs + k, pl.ds(at, cols), :] = place(g, p, k)[...].T
+
+    def await_piece(g, p, k):
+        pltpu.make_async_copy(place(g, p, k), place(g, p, k), recv_sem.at[g, p, k]).wait()
+
+    z_of = (zz,) + nearest
+    home = {
+        "Z": (mine_g, yy), "F": (first_g, first_y),
+        "S": (second_g, second_y), "D": (1 - mine_g, 1 - yy),
+    }
+    twin = {"Z": "Z", "F": "S", "S": "F", "D": "D"}
+
+    def relay(kind, step):
+        g, y = home[kind]
+        p = pq_of(z_of[step], y, core)
+        for k in range(subs):
+            await_piece(g, p, k)
+            if kind == "Z":
+                send(g, p, k, across_peer if step == 1 else beside_peer, middle)
+                send(g, p, k, first_peer)
+            if kind in "ZF":
+                send(g, p, k, second_peer)
+            send(g, p, k, core_peer)
+            flip(g, p, k)
+
+    def take(kind, step):
+        g, y = home[twin[kind]]
+        p = pq_of(z_of[step], y, 1 - core)
+        for k in range(subs):
+            await_piece(g, p, k)
+            flip(g, p, k)
+
+    for k in range(subs):
+        send(mine_g, mine, k, beside_peer)
+        send(mine_g, mine, k, across_peer, middle)
+        send(mine_g, mine, k, first_peer)
+        send(mine_g, mine, k, second_peer)
+    for k in range(subs):
+        send(mine_g, mine, k, core_peer)
+    for k in range(subs):
+        flip(mine_g, mine, k)
+    waves = ("Z1 F0", "S0 Z2 F1", "S1 D0 Z3 F2", "S2 D1 F3", "S3 D2 D3")
+    before = "Z0"
+    for wave in waves:
+        for item in wave.split():
+            relay(item[0], int(item[1]))
+        for item in before.split():
+            take(item[0], int(item[1]))
+        before = wave
+    for item in before.split():
+        take(item[0], int(item[1]))
+    for copy, only in started:
+        if only is None:
+            copy.wait_send()
+        else:
+            pl.when(only)(copy.wait_send)
 
 
 def transform_kernel(
@@ -104,7 +144,7 @@
     pair = 2 * tile
 
     for panel in range(panels):
-        count = count_ref[panel, 0]
+        count = count_ref[panel]
 
         def step(turn, used):
             for k in range(UNROLL):
@@ -155,10 +195,11 @@
     panels, n_z = own.shape[0], own.shape[2]
     f32, bf16 = jnp.float32, jnp.bfloat16
     mine_g, mine = lax.axis_index("grp"), lax.axis_index("pq")
-    core, yy, zz, z_at = coords(mine, n_z)
+    core, yy, zz, nearest, _ = coords(mine)
     core_peer = (mine_g, pq_of(zz, yy, 1 - core))
     y_peer = (mine_g, pq_of(zz, 1 - yy, core))
-    z_peers = [(mine_g, pq_of(z_at(s), yy, core)) for s in range(1, n_z)]
+    far_first = nearest[::-1] + (zz,)
+    z_peers = [(mine_g, pq_of(z, yy, core)) for z in far_first[:-1]]
     meet([core_peer, y_peer] + z_peers)
     sent = []
 
@@ -173,38 +214,35 @@
     def landed(dst, recv):
         pltpu.make_async_copy(dst, dst, recv).wait()
 
-    far_first = list(range(1, n_z)) + [0]
     for y in (1 - yy, yy):
         for panel in range(panels):
             push(other.at[panel, y], from_core.at[panel, y], core_recv.at[panel, y], core_peer)
     for panel in range(panels):
         landed(from_core.at[panel, 1 - yy], core_recv.at[panel, 1 - yy])
-    for s in far_first:
-        z = z_at(s)
+    for s, z in enumerate(far_first):
         for panel in range(panels):
             total = own[panel, 1 - yy, z] + from_core[panel, 1 - yy, z].astype(f32)
             sum_bf[panel, s] = total.astype(bf16)
             push(sum_bf.at[panel, s], from_y.at[panel, s], y_recv.at[panel, s], y_peer)
     for panel in range(panels):
         landed(from_core.at[panel, yy], core_recv.at[panel, yy])
-    for s in far_first:
-        z = z_at(s)
+    for s, z in enumerate(far_first):
         for panel in range(panels):
             landed(from_y.at[panel, s], y_recv.at[panel, s])
             total = (
                 own[panel, yy, z] + from_core[panel, yy, z].astype(f32)
                 + from_y[panel, s].astype(f32)
             )
-            if s:
+            if s < n_z - 1:
                 fin_bf[panel, s] = total.astype(bf16)
-                push(fin_bf.at[panel, s], from_z.at[panel, s], z_recv.at[panel, s], z_peers[s - 1])
+                push(fin_bf.at[panel, s], from_z.at[panel, zz], z_recv.at[panel, zz], z_peers[s])
             else:
                 out_ref[pl.ds(panel * KL_PANEL, KL_PANEL)] = total
     for panel in range(panels):
         total = out_ref[pl.ds(panel * KL_PANEL, KL_PANEL)]
-        for s in range(1, n_z):
-            landed(from_z.at[panel, s], z_recv.at[panel, s])
-            total += from_z[panel, s].astype(f32)
+        for z in nearest:
+            landed(from_z.at[panel, z], z_recv.at[panel, z])
+            total += from_z[panel, z].astype(f32)
         out_ref[pl.ds(panel * KL_PANEL, KL_PANEL)] = total
     for copy in sent:
         copy.wait_send()
@@ -221,13 +259,17 @@
     sems = pltpu.SemaphoreType.DMA
     shape = jax.ShapeDtypeStruct
     mib = 2**20
-    n_gather = 2 + n_z + 3 * (n_z - 1) + 2 * n_z + 2 * n_z
+    subs = rows // tile
+    n_gather = subs * (5 + 4 * (n_z - 1) + 4 * n_z)
     full, flipped = pl.pallas_call(
         functools.partial(gather_kernel, n_grp, n_pq, tile),
         out_shape=(shape((n_grp, nao, cols), bf16), shape((nao // tile, width, tile), bf16)),
-        in_specs=[vmem],
+        in_specs=[pl.BlockSpec(memory_space=pltpu.HBM)],
         out_specs=(vmem, vmem),
-        scratch_shapes=[sems((n_gather,)), sems((n_grp, n_pq))],
+        scratch_shapes=[sems((n_gather,)), sems((n_grp, n_pq, subs)), sems],
+        cost_estimate=pl.CostEstimate(
+            flops=2 * nao * nao * width, bytes_accessed=8 * nao * width, transcendentals=0
+        ),
         compiler_params=pltpu.CompilerParams(
             collective_id=0, has_side_effects=True, vmem_limit_bytes=24 * mib
         ),
@@ -245,7 +287,7 @@
             pltpu.VMEM((width, width), f32),
         ],
         compiler_params=pltpu.CompilerParams(vmem_limit_bytes=40 * mib),
-    )(pair_blocks, block_list, block_count, full, flipped)
+    )(pair_blocks, block_list, block_count.reshape(panels), full, flipped)
     pieces = (panels, n_z, KL_PANEL, chunk, width)
     return pl.pallas_call(
         scatter_kernel,
@@ -311,7 +353,7 @@
     n_grp, n_pq = lax.axis_size("grp"), lax.axis_size("pq")
     rows, cols = coef.shape
     tile = pair_blocks.shape[2]
-    fits = n_grp == 2 and n_pq % 8 == 0 and n_grp * n_pq <= DIRECT_LIMIT
+    fits = n_grp == 2 and n_pq == 4 * LINE
     if fits and rows % tile == 0 and cols % 128 == 0:
         return direct(n_grp, n_pq, pair_blocks, block_list, block_count, coef)
     return gathered(pair_blocks, block_list, block_count, coef)

time: 66 us -> 58.4 us (0.88)
  Pallas kernels: 61.2 us -> 56.7 us
  local copies, waits for them, and re-layouts: 4.29 us -> 1.62 us
    unnamed x8 -> x9, local copies, waits for them, and re-layouts: 4.29 us -> 1.62 us
    pallas_call x1, Pallas kernels: 23.7 us -> 21.1 us  [direct(): pl.pallas_call(scatter_kernel, out_shape=shape((panels * KL_PANEL, chunk,...]
    pallas_call x1, Pallas kernels: 6.74 us -> 5.6 us  [direct(): pl.pallas_call(functools.partial(transform_kernel, n_grp, n_pq), out_shap...]
    pallas_call x1, Pallas kernels: 30.8 us -> 30 us  [direct(): pl.pallas_call(functools.partial(gather_kernel, n_grp, n_pq, tile), out_s...]
where the time goes in v2:
time: 58.4 us
  Pallas kernels  56.7 us (97%)
  local copies, waits for them, and re-layouts  1.62 us (3%)
    pallas_call x1, Pallas kernels, direct(): pl.pallas_call(functools.partial(gather_kernel, n_grp, n_pq, tile), out_s...  30 us
    pallas_call x1, Pallas kernels, direct(): pl.pallas_call(scatter_kernel, out_shape=shape((panels * KL_PANEL, chunk,...  21.1 us
    pallas_call x1, Pallas kernels, direct(): pl.pallas_call(functools.partial(transform_kernel, n_grp, n_pq), out_shap...  5.6 us
    unnamed x9, local copies, waits for them, and re-layouts  1.62 us

profile of v2, /device:TPU:0, one launch (start us, length us, event | category | flops | bytes accessed | tf_op | source)
XLA Modules:
  0.0 58.4 jit_solution(17130441671449281380)
XLA Ops:
  0.0 0.0 copy-start.3
  0.0 0.9 %copy-done.3 = bf16[256,256]{1,0:T(8,128)(2,1)S(1)} copy-done((bf16[256,256]{1,0:T(8,128)(2,1)S(1)}, bf16[256,256]{1,0:T(8,128)(2,1)}, u32[]{:S(2)}) %copy-start.3) | copy-done | bytes 131096
  0.9 0.0 copy-start
  0.9 0.0 copy-start.1
  0.9 0.0 copy-start.2
  0.9 30.0 %shard_map.46 = (bf16[2,4096,256]{2,1,0:T(8,128)(2,1)S(1)}, bf16[32,512,128]{2,1,0:T(8,128)(2,1)S(1)}) custom-call(bf16[256,256]{1,0:T(8,128)(2,1)S(1)} %copy-done.3), custom_call_target="tpu_custom_call" | custom-call | flops 17179869184 | bytes 16777216 | tf_op jit(solution)/shard_map/pallas_call | solution.py:264
  30.9 0.0 copy-done
  30.9 0.0 copy-done.1
  30.9 0.0 copy-done.2
  30.9 5.6 %shard_map.47 = (f32[2,2,4,2,32,512]{5,4,3,2,1,0:T(8,128)S(1)}, bf16[2,2,4,2,32,512]{5,4,3,2,1,0:T(8,128)(2,1)S(1)}) custom-call(bf16[2,18,128,128]{3,2,1,0:T(8,128)(2,1)S(1)} %copy-done, s32[2,18]{1,0:T(2,128)S(1)} %copy-done.1, s32[2]{0:T(128)S(1)} %bitcast.1, bf16[2,4096,256]{2,1,0:T(8,128)(2,1)S(1)} %get-tuple-element.9.full, ...), custom_call_target="tpu_custom_call" | custom-call | tf_op jit(solution)/shard_map/pallas_call | solution.py:279
  36.5 21.1 %shard_map.48 = f32[4,32,512]{2,1,0:T(8,128)S(1)} custom-call(f32[2,2,4,2,32,512]{5,4,3,2,1,0:T(8,128)S(1)} %get-tuple-element.11.own, bf16[2,2,4,2,32,512]{5,4,3,2,1,0:T(8,128)(2,1)S(1)} %get-tuple-element.12.other), custom_call_target="tpu_custom_call" | custom-call | tf_op jit(solution)/shard_map/pallas_call | solution.py:292
  57.7 0.7 %copy.6 = f32[4,32,512]{2,1,0:T(8,128)} copy(f32[4,32,512]{2,1,0:T(8,128)S(1)} %shard_map.48) | data formatting | bytes 524288
Async XLA Ops:
  0.0 0.9 %copy-start.3 = (bf16[256,256]{1,0:T(8,128)(2,1)S(1)}, bf16[256,256]{1,0:T(8,128)(2,1)}, u32[]{:S(2)}) copy-start(bf16[256,256]{1,0:T(8,128)(2,1)} %coef_ref.1) | copy-start | bytes 393220
  0.9 30.0 %copy-start = (bf16[2,18,128,128]{3,2,1,0:T(8,128)(2,1)S(1)}, bf16[2,18,128,128]{3,2,1,0:T(8,128)(2,1)}, u32[]{:S(2)}) copy-start(bf16[2,18,128,128]{3,2,1,0:T(8,128)(2,1)} %blocks_ref.1) | copy-start | bytes 3538948
  0.9 30.0 %copy-start.1 = (s32[2,18]{1,0:T(2,128)S(1)}, s32[2,18]{1,0:T(2,128)}, u32[]{:S(2)}) copy-start(s32[2,18]{1,0:T(2,128)} %list_ref.1) | copy-start | bytes 436
  0.9 30.0 %copy-start.2 = (s32[2,1]{0,1:T(1,128)S(1)}, s32[2,1]{0,1:T(1,128)}, u32[]{:S(2)}) copy-start(s32[2,1]{0,1:T(1,128)} %param.6) | copy-start | bytes 28

commit v3 on v2

--- a/solution.py
+++ b/solution.py
@@ -9,7 +9,7 @@
 
 KL_PANEL = 2
 MESH = pl.DeviceIdType.MESH
-UNROLL = 3
+UNROLL = 6
 
 
 LINE = 4
@@ -116,16 +116,16 @@
         send(mine_g, mine, k, core_peer)
     for k in range(subs):
         flip(mine_g, mine, k)
-    waves = ("Z1 F0", "S0 Z2 F1", "S1 D0 Z3 F2", "S2 D1 F3", "S3 D2 D3")
-    before = "Z0"
-    for wave in waves:
+    waves = ("Z1 F0", "Z2 F1", "S0 Z3 F2", "S1 D0 F3", "S2 D1", "S3 D2 D3")
+    behind = ("", "Z0") + waves
+    for turn, wave in enumerate(waves):
         for item in wave.split():
             relay(item[0], int(item[1]))
-        for item in before.split():
+        for item in behind[turn].split():
             take(item[0], int(item[1]))
-        before = wave
-    for item in before.split():
-        take(item[0], int(item[1]))
+    for wave in behind[len(waves):]:
+        for item in wave.split():
+            take(item[0], int(item[1]))
     for copy, only in started:
         if only is None:
             copy.wait_send()

time: 58.4 us -> 56.3 us (0.964)
  Pallas kernels: 56.7 us -> 54.6 us
    pallas_call x1, Pallas kernels: 21.1 us -> 19.1 us  [direct(): pl.pallas_call(scatter_kernel, out_shape=shape((panels * KL_PANEL, chunk,...]
    pallas_call x1, Pallas kernels: 30 us -> 29.4 us  [direct(): pl.pallas_call(functools.partial(gather_kernel, n_grp, n_pq, tile), out_s...]
where the time goes in v3:
time: 56.3 us; the launch traced here: 56.2 us
  Pallas kernels  54.6 us (97%)
  local copies, waits for them, and re-layouts  1.62 us (3%)
    pallas_call x1, Pallas kernels, direct(): pl.pallas_call(functools.partial(gather_kernel, n_grp, n_pq, tile), out_s...  29.4 us
    pallas_call x1, Pallas kernels, direct(): pl.pallas_call(scatter_kernel, out_shape=shape((panels * KL_PANEL, chunk,...  19.1 us
    pallas_call x1, Pallas kernels, direct(): pl.pallas_call(functools.partial(transform_kernel, n_grp, n_pq), out_shap...  6.08 us
    unnamed x9, local copies, waits for them, and re-layouts  1.62 us

profile of v3, /device:TPU:0, one launch (start us, length us, event | category | flops | bytes accessed | tf_op | source)
XLA Modules:
  0.0 56.2 jit_solution(18354975306866595720)
XLA Ops:
  0.0 0.0 copy-start.3
  0.0 0.9 %copy-done.3 = bf16[256,256]{1,0:T(8,128)(2,1)S(1)} copy-done((bf16[256,256]{1,0:T(8,128)(2,1)S(1)}, bf16[256,256]{1,0:T(8,128)(2,1)}, u32[]{:S(2)}) %copy-start.3) | copy-done | bytes 131096
  0.9 0.0 copy-start
  0.9 0.0 copy-start.1
  0.9 0.0 copy-start.2
  0.9 29.4 %shard_map.46 = (bf16[2,4096,256]{2,1,0:T(8,128)(2,1)S(1)}, bf16[32,512,128]{2,1,0:T(8,128)(2,1)S(1)}) custom-call(bf16[256,256]{1,0:T(8,128)(2,1)S(1)} %copy-done.3), custom_call_target="tpu_custom_call" | custom-call | flops 17179869184 | bytes 16777216 | tf_op jit(solution)/shard_map/pallas_call | solution.py:264
  30.3 0.0 copy-done
  30.3 0.0 copy-done.1
  30.3 0.0 copy-done.2
  30.3 6.1 %shard_map.47 = (f32[2,2,4,2,32,512]{5,4,3,2,1,0:T(8,128)S(1)}, bf16[2,2,4,2,32,512]{5,4,3,2,1,0:T(8,128)(2,1)S(1)}) custom-call(bf16[2,18,128,128]{3,2,1,0:T(8,128)(2,1)S(1)} %copy-done, s32[2,18]{1,0:T(2,128)S(1)} %copy-done.1, s32[2]{0:T(128)S(1)} %bitcast.1, bf16[2,4096,256]{2,1,0:T(8,128)(2,1)S(1)} %get-tuple-element.9.full, ...), custom_call_target="tpu_custom_call" | custom-call | tf_op jit(solution)/shard_map/pallas_call | solution.py:279
  36.4 19.1 %shard_map.48 = f32[4,32,512]{2,1,0:T(8,128)S(1)} custom-call(f32[2,2,4,2,32,512]{5,4,3,2,1,0:T(8,128)S(1)} %get-tuple-element.11.own, bf16[2,2,4,2,32,512]{5,4,3,2,1,0:T(8,128)(2,1)S(1)} %get-tuple-element.12.other), custom_call_target="tpu_custom_call" | custom-call | tf_op jit(solution)/shard_map/pallas_call | solution.py:292
  55.5 0.7 %copy.6 = f32[4,32,512]{2,1,0:T(8,128)} copy(f32[4,32,512]{2,1,0:T(8,128)S(1)} %shard_map.48) | data formatting | bytes 524288
Async XLA Ops:
  0.0 0.9 %copy-start.3 = (bf16[256,256]{1,0:T(8,128)(2,1)S(1)}, bf16[256,256]{1,0:T(8,128)(2,1)}, u32[]{:S(2)}) copy-start(bf16[256,256]{1,0:T(8,128)(2,1)} %coef_ref.1) | copy-start | bytes 393220
  0.9 29.4 %copy-start = (bf16[2,18,128,128]{3,2,1,0:T(8,128)(2,1)S(1)}, bf16[2,18,128,128]{3,2,1,0:T(8,128)(2,1)}, u32[]{:S(2)}) copy-start(bf16[2,18,128,128]{3,2,1,0:T(8,128)(2,1)} %blocks_ref.1) | copy-start | bytes 3538948
  0.9 29.4 %copy-start.1 = (s32[2,18]{1,0:T(2,128)S(1)}, s32[2,18]{1,0:T(2,128)}, u32[]{:S(2)}) copy-start(s32[2,18]{1,0:T(2,128)} %list_ref.1) | copy-start | bytes 436
  0.9 29.4 %copy-start.2 = (s32[2,1]{0,1:T(1,128)S(1)}, s32[2,1]{0,1:T(1,128)}, u32[]{:S(2)}) copy-start(s32[2,1]{0,1:T(1,128)} %param.6) | copy-start | bytes 28
